TPU v7x, 32 devices: a whole 2x2x4 slice. The times are simulated.
32 devices in a mesh: dp: 4 (over y, x), mp: 8 (over z, core).
Axes of the slice: x: 2, y: 2, z: 4, core: 2. Of those that a mesh axis runs over, the one named last changes fastest.
Arguments:
- tokens: bfloat16 [4, 1024, 5120], P('dp', 'mp'), may hold values from -6 to 6
- ln_gain: float32 [5120], replicated, may hold values from 0.1 to 1.9
- ln_bias: float32 [5120], replicated, may hold values from -3 to 3
- w_qkv: bfloat16 [5120, 3, 4096], P(None, None, 'mp'), may hold values from -0.15625 to 0.15625
- w_out: bfloat16 [4096, 5120], P('mp'), may hold values from -0.09375 to 0.09375
- grad_partial: bfloat16 [4, 4096, 5120], P('dp', 'mp'), may hold values from -6 to 6
Outputs:
- mixed: bfloat16 [4, 1024, 5120], P('dp', 'mp')
- grad_sum: float32 [4096, 5120], P('mp')
All inputs are finite; a program needn't handle non-finite values.
Results may differ from a plain program's by a relative error of at most 0.014.
The roundings to bfloat16 on the way count: a program that leaves them out, or rounds other values in their place, can miss the bound.
Values may be sent and summed in bfloat16 or wider, within the bound.
A program may use at most 192 MiB of HBM per device.

v0:
```python
import functools

import jax
import jax.numpy as jnp
from jax import lax
from jax.experimental import pallas as pl
from jax.experimental.pallas import tpu as pltpu
from jax.sharding import PartitionSpec as P

HEAD = 128
SEQ = 128
NORM_ROWS = 16
MESH = pl.DeviceIdType.MESH


def pieces_of(half):
    return next(p for p in (5, 4) if half % (p * 128) == 0)


def kernel(
    n,
    tok_hbm,
    gain,
    bias,
    wq_hbm,
    wo_hbm,
    out_hbm,
    wq,
    wo,
    tok,
    tok_mate,
    blocks,
    theirs,
    stage,
    chain,
    fin,
    out,
    qkv,
    ctx,
    load_sem,
    own_send,
    own_recv,
    up_send,
    up_recv,
    dn_send,
    dn_recv,
    mx_send,
    mx_recv,
    mp_send,
    mp_recv,
    fin_send,
    fin_recv,
):
    chips = n // 2
    slots = 2 * chips
    me = lax.axis_index("mp")
    c = me // 2
    s = me % 2
    mate = c * 2 + 1 - s
    above = me + 2
    below = me - 2
    high = chips - 1 - c
    up = jnp.minimum(high, 1)
    dn = jnp.minimum(c, 1)
    rows, width = tok.shape
    half = width // 2
    pieces = pieces_of(half)
    wide = half // pieces
    inner = wo.shape[0]
    f32 = jnp.float32
    bf16 = jnp.bfloat16

    def remote(src, dst, send, recv, target):
        return pltpu.make_async_remote_copy(
            src_ref=src,
            dst_ref=dst,
            send_sem=send,
            recv_sem=recv,
            device_id={"mp": target},
            device_id_type=MESH,
        )

    def side(h):
        return pl.ds(pl.multiple_of(h * half, 128), half)

    def cols(h, p):
        return pl.ds(pl.multiple_of(h * half + p * wide, 128), wide)

    def sub(p):
        return pl.ds(pl.multiple_of(p * wide, 128), wide)

    def gather_above(a):
        first = a < high
        return jnp.where(first, 2 * (c + 1 + a), 2 * (c + 2 * high - a) + 1)

    def gather_below(a):
        first = a < c
        return jnp.where(first, 2 * (c - 1 - a), 2 * (a - c) + 1)

    def sum_into_up(chip, j):
        first = j < chips + chip
        return jnp.where(first, 2 * (j - chip), 2 * (chip - 1 + slots - j) + 1)

    def sum_into_dn(chip, j):
        mirror = chips - 1 - chip
        first = j < chips + mirror
        t = jnp.where(first, j - mirror, mirror - 1 + slots - j)
        return 2 * (chips - 1 - t) + jnp.where(first, 0, 1)

    def chain_up(chip, j):
        return j - 2 * chip

    def chain_dn(chip, j):
        return 2 * (chips - chip) + j - 2 * (chips - 1 - chip)

    load_t = pltpu.make_async_copy(tok_hbm, tok, load_sem.at[0])
    load_q = pltpu.make_async_copy(wq_hbm, wq, load_sem.at[1])
    load_o = pltpu.make_async_copy(wo_hbm, wo, load_sem.at[2])
    store = pltpu.make_async_copy(out, out_hbm, load_sem.at[3])
    load_t.start()
    load_q.start()
    load_o.start()

    barrier = pltpu.get_barrier_semaphore()
    pl.semaphore_signal(barrier, inc=1, device_id={"mp": mate}, device_id_type=MESH)

    @pl.when(up > 0)
    def _():
        pl.semaphore_signal(barrier, inc=1, device_id={"mp": above}, device_id_type=MESH)

    @pl.when(dn > 0)
    def _():
        pl.semaphore_signal(barrier, inc=1, device_id={"mp": below}, device_id_type=MESH)

    load_t.wait()

    def norm(r, carry):
        here = pl.ds(pl.multiple_of(r * NORM_ROWS, NORM_ROWS), NORM_ROWS)
        values = tok[here, :].astype(f32)
        center = jnp.mean(values, axis=-1, keepdims=True)
        values = values - center
        spread = jnp.mean(values * values, axis=-1, keepdims=True)
        blocks[me, here, :] = (values * lax.rsqrt(spread + 1e-06) * gain[...] + bias[...]).astype(bf16)
        return carry

    lax.fori_loop(0, rows // NORM_ROWS, norm, 0)

    pl.semaphore_wait(barrier, 1 + up + dn)

    def own(slot, h, i):
        at = blocks.at[slot, :, side(h)]
        return remote(at, at, own_send.at[i], own_recv.at[i], mate)

    def raw(h):
        return remote(tok.at[:, side(h)], tok_mate, own_send.at[2], own_recv.at[2], mate)

    own(me, 1 - s, 0).start()
    own(me, s, 1).start()
    raw(1 - s).start()

    def hop_up(slot, j, p):
        at = blocks.at[slot, :, cols(s, p)]
        return remote(at, at, up_send.at[j], up_recv.at[j, p], above)

    def hop_dn(slot, j, p):
        at = blocks.at[slot, :, cols(s, p)]
        return remote(at, at, dn_send.at[j], dn_recv.at[j, p], below)

    def add_up(slot, j, p):
        return remote(
            theirs.at[slot, :, sub(p)],
            chain.at[chain_up(c + 1, j), :, sub(p)],
            up_send.at[j],
            up_recv.at[j, p],
            above,
        )

    def add_dn(slot, j, p):
        return remote(
            theirs.at[slot, :, sub(p)],
            chain.at[chain_dn(c - 1, j), :, sub(p)],
            dn_send.at[j],
            dn_recv.at[j, p],
            below,
        )

    def to_mate(slot, p):
        at = blocks.at[slot, :, cols(s, p)]
        return remote(at, at, mx_send.at[slot], mx_recv.at[slot], mate)

    def from_mate(slot):
        at = blocks.at[slot, :, side(1 - s)]
        return remote(at, at, mx_send.at[slot], mx_recv.at[slot], mate)

    def share(k, slot):
        return remote(stage.at[k], theirs.at[slot], mp_send.at[k], mp_recv.at[slot], mate)

    @pl.when(s == 1)
    def _():
        own(2 * c, s, 0).wait_recv()

    @pl.when(up > 0)
    def _():
        for p in range(pieces):
            hop_up(2 * c, 0, p).start()

    @pl.when(dn > 0)
    def _():
        for p in range(pieces):
            hop_dn(2 * c, 0, p).start()

    @pl.when(s == 0)
    def _():
        own(2 * c + 1, s, 0).wait_recv()

    @pl.when(dn == 0)
    def _():
        chain[chain_up(c, 2 * c), :, :] = jnp.zeros((rows, half), bf16)
        chain[chain_up(c, slots - 1), :, :] = jnp.zeros((rows, half), bf16)

    @pl.when(up == 0)
    def _():
        chain[chain_dn(c, 2 * high), :, :] = jnp.zeros((rows, half), bf16)
        chain[chain_dn(c, slots - 1), :, :] = jnp.zeros((rows, half), bf16)

    own(mate, 1 - s, 1).wait_recv()
    raw(s).wait_recv()
    own(me, 1 - s, 0).wait_send()
    own(me, s, 1).wait_send()
    raw(1 - s).wait_send()
    load_q.wait()
    load_o.wait()

    def project(slot):
        def one(which, carry):
            qkv[which, :, :] = jnp.dot(
                blocks[slot], wq[which], preferred_element_type=f32
            ).astype(bf16)
            return carry

        lax.fori_loop(0, 3, one, 0)

    def attend():
        for image in range(rows // SEQ):
            here = slice(image * SEQ, (image + 1) * SEQ)
            for h in range(inner // HEAD):
                lanes = slice(h * HEAD, (h + 1) * HEAD)
                scores = lax.dot_general(
                    qkv[0, here, lanes],
                    qkv[1, here, lanes],
                    (((1,), (1,)), ((), ())),
                    preferred_element_type=f32,
                ) * HEAD ** (-0.5)
                expsc = jnp.exp(scores - jnp.max(scores, axis=-1, keepdims=True))
                attn = (expsc / jnp.sum(expsc, axis=-1, keepdims=True)).astype(bf16)
                ctx[here, lanes] = jnp.dot(
                    attn, qkv[2, here, lanes], preferred_element_type=f32
                ).astype(bf16)

    block = half // 2

    def output(slot, k):
        for i in range(2):
            at = pl.ds(pl.multiple_of((1 - s) * half + i * block, 128), block)
            stage[k, :, i * block : (i + 1) * block] = jnp.dot(
                ctx[...], wo[:, at], preferred_element_type=f32
            ).astype(bf16)
        share(k, slot).start()
        for i in range(2):
            at = pl.ds(pl.multiple_of(s * half + i * block, 128), block)
            to = pl.ds(pl.multiple_of((1 - s) * half + i * block, 128), block)
            blocks[slot, :, to] = jnp.dot(
                ctx[...], wo[:, at], preferred_element_type=f32
            ).astype(bf16)

    def mine(slot, p):
        return blocks[slot, :, cols(1 - s, p)].astype(f32) + theirs[slot, :, sub(p)].astype(f32)

    def finish(slot, p, foreign):
        value = (
            mine(slot, p)
            + chain[chain_up(c, jnp.where(slot % 2 == 0, 2 * c, slots - 1)), :, sub(p)].astype(f32)
            + chain[chain_dn(c, jnp.where(slot % 2 == 0, 2 * high, slots - 1)), :, sub(p)].astype(f32)
        )
        if foreign:
            fin[:, sub(p)] = (tok_mate[:, sub(p)].astype(f32) + value).astype(bf16)
            give(p).start()
        else:
            out[:, cols(s, p)] = (tok[:, cols(s, p)].astype(f32) + value).astype(bf16)

    def give(p):
        return remote(fin.at[:, sub(p)], out.at[:, cols(s, p)], fin_send.at[p], fin_recv.at[p], mate)

    def take(p):
        return remote(fin.at[:, sub(p)], out.at[:, cols(1 - s, p)], fin_send.at[p], fin_recv.at[p], mate)

    top = 1 - up

    def candidate(j, k):
        a = j - 1
        has_above = jnp.minimum(jnp.maximum(2 * high - a, 0), 1)
        has_below = jnp.minimum(jnp.maximum(2 * c - a, 0), 1)
        from_above = jnp.where(k == 0, 1 - top, 0)
        from_below = jnp.where(k == 0, top, 1 - top)
        later = from_above * has_above + from_below * has_below
        exists = jnp.where(j == 0, 1, later)
        slot = jnp.where(from_above == 1, gather_above(a), gather_below(a))
        return exists, jnp.where(j == 0, 2 * c + k, slot)

    def tick(j, p):
        k = p // 2
        exists, slot = candidate(j, k)
        active = jnp.where(p < 4, exists, 0)

        @pl.when(active * (1 - p % 2) > 0)
        def _():
            @pl.when(j > 0)
            def _():
                from_mate(slot).wait_recv()

            project(slot)

        @pl.when(active * (p % 2) > 0)
        def _():
            attend()
            output(slot, k)

        last = jnp.where(j == slots - 1, 1, 0)

        @pl.when(last * jnp.where(p == 0, 1, 0) > 0)
        def _():
            share(0, 2 * c).wait_recv()
            share(0, 2 * c + 1).wait_recv()
            for ab in range(2):
                @pl.when(s == ab)
                def _():
                    def one(q, carry):
                        finish(2 * c, q, ab == 1)
                        return carry

                    lax.fori_loop(0, pieces, one, 0)

        @pl.when(dn > 0)
        def _():
            @pl.when(j < 2 * c)
            def _():
                image = gather_below(j)
                hop_up(image, j, p).wait_recv()

                @pl.when(up > 0)
                def _():
                    hop_up(image, j + 1, p).start()

                to_mate(image, p).start()

            @pl.when(j >= 2 * c)
            def _():
                image = sum_into_up(c, j)
                at = chain_up(c, j)
                remote(
                    theirs.at[image, :, sub(p)],
                    chain.at[at, :, sub(p)],
                    up_send.at[j],
                    up_recv.at[j, p],
                    above,
                ).wait_recv()

                @pl.when(image >= 2 * c + 2)
                def _():
                    @pl.when(p == 0)
                    def _():
                        share(0, image).wait_recv()

                    theirs[image, :, sub(p)] = (
                        mine(image, p) + chain[at, :, sub(p)].astype(f32)
                    ).astype(bf16)
                    add_up(image, j + 1, p).start()

        @pl.when(up > 0)
        def _():
            @pl.when(j < 2 * high)
            def _():
                image = gather_above(j)
                hop_dn(image, j, p).wait_recv()

                @pl.when(dn > 0)
                def _():
                    hop_dn(image, j + 1, p).start()

                to_mate(image, p).start()

            @pl.when(j >= 2 * high)
            def _():
                image = sum_into_dn(c, j)
                at = chain_dn(c, j)
                remote(
                    theirs.at[image, :, sub(p)],
                    chain.at[at, :, sub(p)],
                    dn_send.at[j],
                    dn_recv.at[j, p],
                    below,
                ).wait_recv()

                @pl.when(image < 2 * c)
                def _():
                    @pl.when(p == 0)
                    def _():
                        share(0, image).wait_recv()

                    theirs[image, :, sub(p)] = (
                        mine(image, p) + chain[at, :, sub(p)].astype(f32)
                    ).astype(bf16)
                    add_dn(image, j + 1, p).start()

        @pl.when(up * jnp.where(p == 0, 1, 0) * jnp.where(j == 2 * c, 1, 0) > 0)
        def _():
            for q in range(pieces):
                hop_up(2 * c + 1, 2 * c + 1, q).start()

        @pl.when(dn * jnp.where(p == 0, 1, 0) * jnp.where(j == 2 * high, 1, 0) > 0)
        def _():
            for q in range(pieces):
                hop_dn(2 * c + 1, 2 * high + 1, q).start()

        begin = jnp.where(p == 3, 1, 0) * jnp.minimum(j, 1) * (1 - last)

        @pl.when(begin * (1 - dn) * up > 0)
        def _():
            image = sum_into_up(c + 1, j + 1)
            share(0, image).wait_recv()

            def one(q, carry):
                theirs[image, :, sub(q)] = mine(image, q).astype(bf16)
                add_up(image, j + 1, q).start()
                return carry

            lax.fori_loop(0, pieces, one, 0)

        @pl.when(begin * (1 - up) * dn > 0)
        def _():
            image = sum_into_dn(c - 1, j + 1)
            share(0, image).wait_recv()

            def one(q, carry):
                theirs[image, :, sub(q)] = mine(image, q).astype(bf16)
                add_dn(image, j + 1, q).start()
                return carry

            lax.fori_loop(0, pieces, one, 0)

        for ab in range(2):
            @pl.when(last * jnp.where(s == ab, 1, 0) > 0)
            def _():
                finish(2 * c + 1, p, ab == 0)

        @pl.when(p == pieces - 1)
        def _():
            for b in range(2):
                there, image = candidate(j, b)

                @pl.when(there > 0)
                def _():
                    share(b, image).wait_send()

    def slot_loop(j, carry):
        def piece_loop(p, inside):
            tick(j, p)
            return inside

        return lax.fori_loop(0, pieces, piece_loop, carry)

    lax.fori_loop(0, slots, slot_loop, 0)

    for p in range(pieces):
        take(p).wait_recv()
    store.start()

    def drain(j, carry):
        @pl.when(up > 0)
        def _():
            remote(
                blocks.at[0, :, side(s)], blocks.at[0, :, side(s)], up_send.at[j], up_recv.at[0, 0], above
            ).wait_send()

        @pl.when(dn > 0)
        def _():
            remote(
                blocks.at[0, :, side(s)], blocks.at[0, :, side(s)], dn_send.at[j], dn_recv.at[0, 0], below
            ).wait_send()

        @pl.when(j // 2 != c)
        def _():
            from_mate(j).wait_send()

        return carry

    lax.fori_loop(0, slots, drain, 0)
    for p in range(pieces):
        give(p).wait_send()
    store.wait()


def body(n, tokens, ln_gain, ln_bias, w_qkv, w_out, grad_partial):
    local_rows = tokens[0]
    rows, width = local_rows.shape
    inner = w_out.shape[0]
    chips = n // 2
    slots = 2 * chips
    half = width // 2
    pieces = pieces_of(half)
    dma = pltpu.SemaphoreType.DMA
    flops = 2 * rows * n * width * inner * 4
    vmem = pl.BlockSpec(memory_space=pltpu.VMEM)
    hbm = pl.BlockSpec(memory_space=pl.ANY)
    mixed = pl.pallas_call(
        functools.partial(kernel, n),
        out_shape=jax.ShapeDtypeStruct((rows, width), jnp.bfloat16),
        in_specs=[hbm, vmem, vmem, hbm, hbm],
        out_specs=hbm,
        scratch_shapes=[
            pltpu.VMEM((3, width, inner), jnp.bfloat16),
            pltpu.VMEM((inner, width), jnp.bfloat16),
            pltpu.VMEM((rows, width), jnp.bfloat16),
            pltpu.VMEM((rows, half), jnp.bfloat16),
            pltpu.VMEM((n, rows, width), jnp.bfloat16),
            pltpu.VMEM((n, rows, half), jnp.bfloat16),
            pltpu.VMEM((2, rows, half), jnp.bfloat16),
            pltpu.VMEM((slots + 2, rows, half), jnp.bfloat16),
            pltpu.VMEM((rows, half), jnp.bfloat16),
            pltpu.VMEM((rows, width), jnp.bfloat16),
            pltpu.VMEM((3, rows, inner), jnp.bfloat16),
            pltpu.VMEM((rows, inner), jnp.bfloat16),
            dma((4,)),
            dma((3,)),
            dma((3,)),
            dma((slots,)),
            dma((slots, pieces)),
            dma((slots,)),
            dma((slots, pieces)),
            dma((n,)),
            dma((n,)),
            dma((2,)),
            dma((n,)),
            dma((pieces,)),
            dma((pieces,)),
        ],
        compiler_params=pltpu.CompilerParams(
            collective_id=0, has_side_effects=True, vmem_limit_bytes=66_000_000
        ),
        cost_estimate=pl.CostEstimate(
            flops=flops * 8, bytes_accessed=300_000_000, transcendentals=0
        ),
    )(
        local_rows,
        ln_gain.reshape(1, width),
        ln_bias.reshape(1, width),
        jnp.transpose(w_qkv, (1, 0, 2)),
        w_out,
    )[None]
    grad_sum = lax.psum(grad_partial[0], "dp").astype(jnp.float32)
    return (mixed, grad_sum)


def solution(mesh):
    placed = (
        P("dp", "mp", None),
        P(),
        P(),
        P(None, None, "mp"),
        P("mp", None),
        P("dp", "mp", None),
    )
    return jax.shard_map(
        functools.partial(body, mesh.shape["mp"]),
        mesh=mesh,
        in_specs=placed,
        out_specs=(P("dp", "mp", None), P("mp", None)),
        check_vma=False,
    )
```

profile of v0, /device:TPU:0, one launch (start us, length us, event | category | flops | bytes accessed | tf_op | source)
XLA Modules:
  0.0 150.9 jit_solution(2628504648584105078)
XLA Ops:
  7.2 0.0 all-reduce.2.cloned.1.call-start
  7.2 0.7 all-reduce.2.cloned.1.call-update
  7.9 122.7 %shard_map.77 = bf16[128,5120]{1,0:T(8,128)(2,1)} custom-call(bf16[128,5120]{1,0:T(8,128)(2,1)} %bitcast.9, f32[1,5120]{1,0:T(1,128)} %bitcast.10, f32[1,5120]{1,0:T(1,128)} %bitcast.11, bf16[3,5120,512]{2,1,0:T(8,128)(2,1)} %bitcast.8, bf16[512,5120]{1,0:T(8,128)(2,1)} %wo_hbm.1), custom_call_target="tpu_custom_call" | custom-call | flops 171798691840 | bytes 300000000 | tf_op jit(solution)/shard_map/pallas_call | solution.py:515
  130.6 0.0 copy-start
  130.6 4.4 %all-reduce.2.cloned.1.call-done = bf16[512,5120]{1,0:T(8,128)(2,1)} async-done(((bf16[512,5120]{1,0:T(8,128)(2,1)}), bf16[512,5120]{1,0:T(8,128)(2,1)}) %all-reduce.2.cloned.1.call-update) | async-done | bytes 5242896 | tf_op jit(solution)/shard_map/psum | solution.py:560
  135.1 7.9 %convert_element_type.3 = f32[512,5120]{1,0:T(8,128)} convert(bf16[512,5120]{1,0:T(8,128)(2,1)} %all-reduce.2.cloned.1.call-done) | non-fusion elementwise | flops 2621440 | bytes 15728640 | tf_op jit(solution)/shard_map/convert_element_type | solution.py:560
  143.0 0.0 copy-done
  143.0 1.1 copy.11
Async XLA Ops:
  7.2 127.9 %all-reduce.2.cloned.1.call-start = ((), (), s32[]{:S(2)}) async-start(), calls=%async_computation | async-start | bytes 10485760 | tf_op jit(solution)/shard_map/psum | solution.py:560
  130.6 12.4 %copy-start = (bf16[128,5120]{1,0:T(8,128)(2,1)S(1)}, bf16[128,5120]{1,0:T(8,128)(2,1)}, u32[]{:S(2)}) copy-start(bf16[128,5120]{1,0:T(8,128)(2,1)} %shard_map.77) | copy-start | bytes 3932164
Sparse Core Ops, SparseCore 0:
  11.3 123.7 all-reduce.1
where the time goes:
time: 151 us
  Pallas kernels  123 us (81%)
  between operations  14 us (9%)
  other arithmetic  7.93 us (5%)
  waiting for transfers between devices  5.12 us (3%)
    pallas_call x1, Pallas kernels, body(): pl.pallas_call(functools.partial(kernel, n), out_shape=jax.ShapeDtypeStru...  123 us
    convert_element_type x1, other arithmetic, body(): grad_sum = lax.psum(grad_partial[0], 'dp').astype(jnp.float32)  7.93 us
    psum x1, waiting for transfers between devices, body(): grad_sum = lax.psum(grad_partial[0], 'dp').astype(jnp.float32)  4.44 us
  transfers between devices with their start and end apart: 1, of which 1 were waited for; matrix products, arithmetic and copies ran while one was open for 0% of the time, Pallas kernels for 81%

commit v1 on v0

--- a/solution.py
+++ b/solution.py
@@ -19,12 +19,15 @@
 
 def kernel(
     n,
+    groups,
     tok_hbm,
     gain,
     bias,
     wq_hbm,
     wo_hbm,
-    out_hbm,
+    grad_hbm,
+    out,
+    total,
     wq,
     wo,
     tok,
@@ -34,9 +37,9 @@
     stage,
     chain,
     fin,
-    out,
     qkv,
     ctx,
+    income,
     load_sem,
     own_send,
     own_recv,
@@ -50,7 +53,14 @@
     mp_recv,
     fin_send,
     fin_recv,
+    rs_send,
+    rs_recv,
+    ag_send,
+    ag_recv,
 ):
+    bits = groups.bit_length() - 1
+    assert groups == 1 << bits
+    group = lax.axis_index("dp")
     chips = n // 2
     slots = 2 * chips
     me = lax.axis_index("mp")
@@ -116,11 +126,126 @@
     load_t = pltpu.make_async_copy(tok_hbm, tok, load_sem.at[0])
     load_q = pltpu.make_async_copy(wq_hbm, wq, load_sem.at[1])
     load_o = pltpu.make_async_copy(wo_hbm, wo, load_sem.at[2])
-    store = pltpu.make_async_copy(out, out_hbm, load_sem.at[3])
     load_t.start()
     load_q.start()
     load_o.start()
 
+    grows = grad_hbm.shape[0] // 2
+
+    def partner(h, i):
+        bit = 1 << (i if h == 0 else bits - 1 - i)
+        side_of = (group // bit) % 2
+        return group + bit * (1 - 2 * side_of), side_of
+
+    def region(h, i):
+        base = h * grows
+        size = grows
+        for step in range(i + 1):
+            size = size // 2
+            if step < i:
+                base = base + partner(h, step)[1] * size
+        keep = partner(h, i)[1]
+        return base + keep * size, base + (1 - keep) * size, size
+
+    offset = [0]
+    for step in range(bits):
+        offset.append(offset[-1] + (grows >> (step + 1)))
+
+    def span(base, size):
+        return pl.ds(pl.multiple_of(base, 16), size)
+
+    def scatter(h, i):
+        _, away, size = region(h, i)
+        if i == 0:
+            source = grad_hbm.at[span(away, size), :]
+        else:
+            source = income.at[h, span(offset[i - 1] + away - region(h, i - 1)[0], size), :]
+        return pltpu.make_async_remote_copy(
+            src_ref=source,
+            dst_ref=income.at[h, offset[i] : offset[i] + size, :],
+            send_sem=rs_send.at[h, i],
+            recv_sem=rs_recv.at[h, i],
+            device_id={"dp": partner(h, i)[0]},
+            device_id_type=MESH,
+        )
+
+    def collect(h, i):
+        keep, _, size = region(h, i)
+        at = total.at[span(keep, size), :]
+        return pltpu.make_async_remote_copy(
+            src_ref=at,
+            dst_ref=at,
+            send_sem=ag_send.at[h, i],
+            recv_sem=ag_recv.at[h, i],
+            device_id={"dp": partner(h, i)[0]},
+            device_id_type=MESH,
+        )
+
+    def collected(h, i):
+        _, away, size = region(h, i)
+        at = total.at[span(away, size), :]
+        return pltpu.make_async_remote_copy(
+            src_ref=at,
+            dst_ref=at,
+            send_sem=ag_send.at[h, i],
+            recv_sem=ag_recv.at[h, i],
+            device_id={"dp": partner(h, i)[0]},
+            device_id_type=MESH,
+        )
+
+    def load_g(h):
+        keep, _, size = region(h, 0)
+        return pltpu.make_async_copy(
+            grad_hbm.at[span(keep, size), :], total.at[span(keep, size), :], load_sem.at[3 + h]
+        )
+
+    for h in range(2):
+        load_g(h).start()
+
+    def grad_event(e):
+        for h in range(2):
+            if e < bits:
+                if e == 0:
+                    load_g(h).wait()
+                scatter(h, e).wait_recv()
+                keep, _, size = region(h, e)
+
+                def add(base, count, leaves):
+                    def one(r, carry):
+                        here = span(base + r * 16, 16)
+                        there = span(offset[e] + base - keep + r * 16, 16)
+                        both = total[here, :].astype(f32) + income[h, there, :].astype(f32)
+                        if leaves:
+                            income[h, there, :] = both.astype(bf16)
+                        else:
+                            total[here, :] = both.astype(bf16)
+                        return carry
+
+                    lax.fori_loop(0, count // 16, one, 0)
+
+                if e + 1 < bits:
+                    stay, leave, count = region(h, e + 1)
+                    add(leave, count, True)
+                    scatter(h, e + 1).start()
+                    add(stay, count, False)
+                else:
+                    add(keep, size, False)
+                    collect(h, e).start()
+            else:
+                i = 2 * bits - 1 - e
+                collected(h, i).wait_recv()
+                if i > 0:
+                    collect(h, i - 1).start()
+
+
+    times = []
+    at_tick = 0
+    for e in range(2 * bits):
+        step = e if e < bits else 2 * bits - 1 - e
+        lines = (grows >> (step + 1)) * width
+        at_tick += -(-lines // (rows * wide)) + 1
+        times.append(min(at_tick, slots * pieces - 2 * bits + e))
+
     barrier = pltpu.get_barrier_semaphore()
     pl.semaphore_signal(barrier, inc=1, device_id={"mp": mate}, device_id_type=MESH)
 
@@ -131,6 +256,11 @@
     @pl.when(dn > 0)
     def _():
         pl.semaphore_signal(barrier, inc=1, device_id={"mp": below}, device_id_type=MESH)
+
+    for i in range(bits):
+        pl.semaphore_signal(
+            barrier, inc=1, device_id={"dp": partner(0, i)[0]}, device_id_type=MESH
+        )
 
     load_t.wait()
 
@@ -145,7 +275,7 @@
 
     lax.fori_loop(0, rows // NORM_ROWS, norm, 0)
 
-    pl.semaphore_wait(barrier, 1 + up + dn)
+    pl.semaphore_wait(barrier, 1 + up + dn + bits)
 
     def own(slot, h, i):
         at = blocks.at[slot, :, side(h)]
@@ -208,6 +338,9 @@
     def _():
         for p in range(pieces):
             hop_dn(2 * c, 0, p).start()
+
+    for h in range(2):
+        scatter(h, 0).start()
 
     @pl.when(s == 0)
     def _():
@@ -453,6 +586,11 @@
             def _():
                 finish(2 * c + 1, p, ab == 0)
 
+        for e, when in enumerate(times):
+            @pl.when(j * pieces + p == when)
+            def _():
+                grad_event(e)
+
         @pl.when(p == pieces - 1)
         def _():
             for b in range(2):
@@ -473,7 +611,6 @@
 
     for p in range(pieces):
         take(p).wait_recv()
-    store.start()
 
     def drain(j, carry):
         @pl.when(up > 0)
@@ -497,40 +634,74 @@
     lax.fori_loop(0, slots, drain, 0)
     for p in range(pieces):
         give(p).wait_send()
-    store.wait()
-
-
-def body(n, tokens, ln_gain, ln_bias, w_qkv, w_out, grad_partial):
+    for h in range(2):
+        for i in range(bits):
+            scatter(h, i).wait_send()
+            collect(h, i).wait_send()
+
+
+def spread(mixed, total, mixed_hbm, total_hbm, wide, sem):
+    parts = wide.shape[0]
+    rows = wide.shape[1]
+    first = pltpu.make_async_copy(mixed, mixed_hbm, sem.at[parts])
+    first.start()
+
+    def put(i):
+        at = pl.ds(pl.multiple_of(i * rows, 8), rows)
+        return pltpu.make_async_copy(wide.at[i], total_hbm.at[at, :], sem.at[i])
+
+    def one(i, carry):
+        at = pl.ds(pl.multiple_of(i * rows, 8), rows)
+        wide[i, :, :] = total[at, :].astype(jnp.float32)
+        put(i).start()
+        return carry
+
+    lax.fori_loop(0, parts, one, 0)
+
+    def done(i, carry):
+        put(i).wait()
+        return carry
+
+    lax.fori_loop(0, parts, done, 0)
+    first.wait()
+
+
+def body(n, groups, tokens, ln_gain, ln_bias, w_qkv, w_out, grad_partial):
     local_rows = tokens[0]
     rows, width = local_rows.shape
     inner = w_out.shape[0]
+    grows = grad_partial.shape[1]
     chips = n // 2
     slots = 2 * chips
+    bits = groups.bit_length() - 1
     half = width // 2
     pieces = pieces_of(half)
     dma = pltpu.SemaphoreType.DMA
     flops = 2 * rows * n * width * inner * 4
     vmem = pl.BlockSpec(memory_space=pltpu.VMEM)
     hbm = pl.BlockSpec(memory_space=pl.ANY)
-    mixed = pl.pallas_call(
-        functools.partial(kernel, n),
-        out_shape=jax.ShapeDtypeStruct((rows, width), jnp.bfloat16),
-        in_specs=[hbm, vmem, vmem, hbm, hbm],
-        out_specs=hbm,
+    bf16 = jnp.bfloat16
+    results = (rows + grows) * width * 2
+    income = sum(grows >> (i + 2) for i in range(bits))
+    mixed, total = pl.pallas_call(
+        functools.partial(kernel, n, groups),
+        out_shape=(pltpu.VMEM((rows, width), bf16), pltpu.VMEM((grows, width), bf16)),
+        in_specs=[hbm, vmem, vmem, hbm, hbm, hbm],
+        out_specs=(vmem, vmem),
         scratch_shapes=[
-            pltpu.VMEM((3, width, inner), jnp.bfloat16),
-            pltpu.VMEM((inner, width), jnp.bfloat16),
-            pltpu.VMEM((rows, width), jnp.bfloat16),
-            pltpu.VMEM((rows, half), jnp.bfloat16),
-            pltpu.VMEM((n, rows, width), jnp.bfloat16),
-            pltpu.VMEM((n, rows, half), jnp.bfloat16),
-            pltpu.VMEM((2, rows, half), jnp.bfloat16),
-            pltpu.VMEM((slots + 2, rows, half), jnp.bfloat16),
-            pltpu.VMEM((rows, half), jnp.bfloat16),
-            pltpu.VMEM((rows, width), jnp.bfloat16),
-            pltpu.VMEM((3, rows, inner), jnp.bfloat16),
-            pltpu.VMEM((rows, inner), jnp.bfloat16),
-            dma((4,)),
+            pltpu.VMEM((3, width, inner), bf16),
+            pltpu.VMEM((inner, width), bf16),
+            pltpu.VMEM((rows, width), bf16),
+            pltpu.VMEM((rows, half), bf16),
+            pltpu.VMEM((n, rows, width), bf16),
+            pltpu.VMEM((n, rows, half), bf16),
+            pltpu.VMEM((2, rows, half), bf16),
+            pltpu.VMEM((slots + 2, rows, half), bf16),
+            pltpu.VMEM((rows, half), bf16),
+            pltpu.VMEM((3, rows, inner), bf16),
+            pltpu.VMEM((rows, inner), bf16),
+            pltpu.VMEM((2, income, width), bf16),
+            dma((5,)),
             dma((3,)),
             dma((3,)),
             dma((slots,)),
@@ -543,9 +714,13 @@
             dma((n,)),
             dma((pieces,)),
             dma((pieces,)),
+            dma((2, bits)),
+            dma((2, bits)),
+            dma((2, bits)),
+            dma((2, bits)),
         ],
         compiler_params=pltpu.CompilerParams(
-            collective_id=0, has_side_effects=True, vmem_limit_bytes=66_000_000
+            collective_id=0, has_side_effects=True, vmem_limit_bytes=66_900_000 - results
         ),
         cost_estimate=pl.CostEstimate(
             flops=flops * 8, bytes_accessed=300_000_000, transcendentals=0
@@ -556,9 +731,27 @@
         ln_bias.reshape(1, width),
         jnp.transpose(w_qkv, (1, 0, 2)),
         w_out,
-    )[None]
-    grad_sum = lax.psum(grad_partial[0], "dp").astype(jnp.float32)
-    return (mixed, grad_sum)
+        grad_partial[0],
+    )
+    parts = grows // 32
+    mixed, grad_sum = pl.pallas_call(
+        spread,
+        out_shape=(
+            jax.ShapeDtypeStruct((rows, width), bf16),
+            jax.ShapeDtypeStruct((grows, width), jnp.float32),
+        ),
+        in_specs=[vmem, vmem],
+        out_specs=(hbm, hbm),
+        scratch_shapes=[
+            pltpu.VMEM((parts, grows // parts, width), jnp.float32),
+            dma((parts + 1,)),
+        ],
+        compiler_params=pltpu.CompilerParams(vmem_limit_bytes=grows * width * 4 + 2_000_000),
+        cost_estimate=pl.CostEstimate(
+            flops=grows * width, bytes_accessed=grows * width * 6, transcendentals=0
+        ),
+    )(mixed, total)
+    return (mixed[None], grad_sum)
 
 
 def solution(mesh):
@@ -571,7 +764,7 @@
         P("dp", "mp", None),
     )
     return jax.shard_map(
-        functools.partial(body, mesh.shape["mp"]),
+        functools.partial(body, mesh.shape["mp"], mesh.shape["dp"]),
         mesh=mesh,
         in_specs=placed,
         out_specs=(P("dp", "mp", None), P("mp", None)),

time: 151 us -> 128 us (0.85)
  between operations: 14 us -> 0.64 us
  other arithmetic: 7.93 us -> 0 us
  waiting for transfers between devices: 5.12 us -> 0 us
  Pallas kernels: 123 us -> 127 us
    convert_element_type x1 -> x0, other arithmetic: 7.93 us -> none  [body(): grad_sum = lax.psum(grad_partial[0], 'dp').astype(jnp.float32)]
    pallas_call x1 -> x2, Pallas kernels: 123 us -> 127 us  [the longest x1 123 us: body(): pl.pallas_call(functools.partial(kernel, n, groups), out_shape=(pltpu.VME...]
    psum x1 -> x0, waiting for transfers between devices: 4.44 us -> none  [body(): grad_sum = lax.psum(grad_partial[0], 'dp').astype(jnp.float32)]
  transfers between devices with their start and end apart: 1 -> 0, of which waited for: 1 -> 0; matrix products, arithmetic and copies ran while one was open for 0% -> 0% of each run, Pallas kernels for 81% -> 0%
where the time goes in v1:
time: 128 us
  Pallas kernels  127 us (99%)
    pallas_call x1, Pallas kernels, body(): pl.pallas_call(functools.partial(kernel, n, groups), out_shape=(pltpu.VME...  123 us
    pallas_call x1, Pallas kernels, body(): pl.pallas_call(spread, out_shape=(jax.ShapeDtypeStruct((rows, width), bf1...  4.47 us

profile of v1, /device:TPU:0, one launch (start us, length us, event | category | flops | bytes accessed | tf_op | source)
XLA Modules:
  0.0 127.9 jit_solution(14213778197241436716)
XLA Ops:
  0.6 122.7 %shard_map.77 = (bf16[128,5120]{1,0:T(8,128)(2,1)S(1)}, bf16[512,5120]{1,0:T(8,128)(2,1)S(1)}) custom-call(bf16[128,5120]{1,0:T(8,128)(2,1)} %bitcast.8, f32[1,5120]{1,0:T(1,128)} %bitcast.10, f32[1,5120]{1,0:T(1,128)} %bitcast.11, bf16[3,5120,512]{2,1,0:T(8,128)(2,1)} %bitcast.6, bf16[512,5120]{1,0:T(8,128)(2,1)} %wo_hbm.1, bf16[512,5120]{1,0:T(8,128)(2,1)} %bitcast.7), custom_call_target="tpu_custom_call" | custom-call | flops 171798691840 | bytes 300000000 | tf_op jit(solution)/shard_map/pallas_call | solution.py:686
  123.4 4.5 %shard_map.78 = (bf16[128,5120]{1,0:T(8,128)(2,1)}, f32[512,5120]{1,0:T(8,128)}) custom-call(bf16[128,5120]{1,0:T(8,128)(2,1)S(1)} %get-tuple-element.6.mixed, bf16[512,5120]{1,0:T(8,128)(2,1)S(1)} %get-tuple-element.7.total), custom_call_target="tpu_custom_call" | custom-call | flops 2621440 | bytes 15728640 | tf_op jit(solution)/shard_map/pallas_call | solution.py:737

commit v2 on v1

--- a/solution.py
+++ b/solution.py
@@ -14,7 +14,7 @@
 
 
 def pieces_of(half):
-    return next(p for p in (5, 4) if half % (p * 128) == 0)
+    return next(p for p in (4, 5) if half % (p * 128) == 0)
 
 
 def kernel(
@@ -127,8 +127,6 @@
     load_q = pltpu.make_async_copy(wq_hbm, wq, load_sem.at[1])
     load_o = pltpu.make_async_copy(wo_hbm, wo, load_sem.at[2])
     load_t.start()
-    load_q.start()
-    load_o.start()
 
     grows = grad_hbm.shape[0] // 2
 
@@ -199,9 +197,6 @@
             grad_hbm.at[span(keep, size), :], total.at[span(keep, size), :], load_sem.at[3 + h]
         )
 
-    for h in range(2):
-        load_g(h).start()
-
     def grad_event(e):
         for h in range(2):
             if e < bits:
@@ -263,37 +258,49 @@
         )
 
     load_t.wait()
-
-    def norm(r, carry):
-        here = pl.ds(pl.multiple_of(r * NORM_ROWS, NORM_ROWS), NORM_ROWS)
-        values = tok[here, :].astype(f32)
-        center = jnp.mean(values, axis=-1, keepdims=True)
-        values = values - center
-        spread = jnp.mean(values * values, axis=-1, keepdims=True)
-        blocks[me, here, :] = (values * lax.rsqrt(spread + 1e-06) * gain[...] + bias[...]).astype(bf16)
-        return carry
-
-    lax.fori_loop(0, rows // NORM_ROWS, norm, 0)
-
-    pl.semaphore_wait(barrier, 1 + up + dn + bits)
-
-    def own(slot, h, i):
+    load_q.start()
+    load_o.start()
+    for h in range(2):
+        load_g(h).start()
+
+    strip = rows // pieces
+
+    def lines(p):
+        return pl.ds(pl.multiple_of(p * strip, 16), strip)
+
+    def norm(p):
+        def one(r, carry):
+            at = pl.multiple_of(p * strip + r * NORM_ROWS, NORM_ROWS)
+            here = pl.ds(at, NORM_ROWS)
+            values = tok[here, :].astype(f32)
+            center = jnp.mean(values, axis=-1, keepdims=True)
+            values = values - center
+            spread = jnp.mean(values * values, axis=-1, keepdims=True)
+            scaled = values * lax.rsqrt(spread + 1e-06) * gain[...] + bias[...]
+            blocks[me, here, :] = scaled.astype(bf16)
+            return carry
+
+        lax.fori_loop(0, strip // NORM_ROWS, one, 0)
+
+    def own(slot, h, p):
+        at = blocks.at[slot, lines(p), side(h)]
+        return remote(at, at, own_send.at[p], own_recv.at[p], mate)
+
+    def rest(slot, h):
         at = blocks.at[slot, :, side(h)]
-        return remote(at, at, own_send.at[i], own_recv.at[i], mate)
+        return remote(at, at, own_send.at[pieces], own_recv.at[pieces], mate)
 
     def raw(h):
-        return remote(tok.at[:, side(h)], tok_mate, own_send.at[2], own_recv.at[2], mate)
-
-    own(me, 1 - s, 0).start()
-    own(me, s, 1).start()
-    raw(1 - s).start()
+        return remote(
+            tok.at[:, side(h)], tok_mate, own_send.at[pieces + 1], own_recv.at[pieces + 1], mate
+        )
 
     def hop_up(slot, j, p):
-        at = blocks.at[slot, :, cols(s, p)]
+        at = blocks.at[slot, lines(p), side(s)]
         return remote(at, at, up_send.at[j], up_recv.at[j, p], above)
 
     def hop_dn(slot, j, p):
-        at = blocks.at[slot, :, cols(s, p)]
+        at = blocks.at[slot, lines(p), side(s)]
         return remote(at, at, dn_send.at[j], dn_recv.at[j, p], below)
 
     def add_up(slot, j, p):
@@ -315,7 +322,7 @@
         )
 
     def to_mate(slot, p):
-        at = blocks.at[slot, :, cols(s, p)]
+        at = blocks.at[slot, lines(p), side(s)]
         return remote(at, at, mx_send.at[slot], mx_recv.at[slot], mate)
 
     def from_mate(slot):
@@ -325,26 +332,47 @@
     def share(k, slot):
         return remote(stage.at[k], theirs.at[slot], mp_send.at[k], mp_recv.at[slot], mate)
 
-    @pl.when(s == 1)
-    def _():
-        own(2 * c, s, 0).wait_recv()
-
-    @pl.when(up > 0)
-    def _():
-        for p in range(pieces):
+    def first_hops(p):
+        @pl.when(up > 0)
+        def _():
             hop_up(2 * c, 0, p).start()
 
-    @pl.when(dn > 0)
-    def _():
-        for p in range(pieces):
+        @pl.when(dn > 0)
+        def _():
             hop_dn(2 * c, 0, p).start()
 
+    norm(0)
+    pl.semaphore_wait(barrier, 1 + up + dn + bits)
     for h in range(2):
         scatter(h, 0).start()
 
-    @pl.when(s == 0)
-    def _():
-        own(2 * c + 1, s, 0).wait_recv()
+    def opening(p, carry):
+        @pl.when(p > 0)
+        def _():
+            norm(p)
+
+        own(me, 1 - s, p).start()
+
+        @pl.when(s == 0)
+        def _():
+            first_hops(p)
+
+        return carry
+
+    lax.fori_loop(0, pieces, opening, 0)
+    rest(me, s).start()
+    raw(1 - s).start()
+
+    def opening_mate(p, carry):
+        own(mate, s, p).wait_recv()
+
+        @pl.when(s == 1)
+        def _():
+            first_hops(p)
+
+        return carry
+
+    lax.fori_loop(0, pieces, opening_mate, 0)
 
     @pl.when(dn == 0)
     def _():
@@ -356,10 +384,11 @@
         chain[chain_dn(c, 2 * high), :, :] = jnp.zeros((rows, half), bf16)
         chain[chain_dn(c, slots - 1), :, :] = jnp.zeros((rows, half), bf16)
 
-    own(mate, 1 - s, 1).wait_recv()
+    rest(mate, 1 - s).wait_recv()
     raw(s).wait_recv()
-    own(me, 1 - s, 0).wait_send()
-    own(me, s, 1).wait_send()
+    for p in range(pieces):
+        own(me, 1 - s, p).wait_send()
+    rest(me, s).wait_send()
     raw(1 - s).wait_send()
     load_q.wait()
     load_o.wait()
@@ -702,8 +731,8 @@
             pltpu.VMEM((rows, inner), bf16),
             pltpu.VMEM((2, income, width), bf16),
             dma((5,)),
-            dma((3,)),
-            dma((3,)),
+            dma((pieces + 2,)),
+            dma((pieces + 2,)),
             dma((slots,)),
             dma((slots, pieces)),
             dma((slots,)),
@@ -733,7 +762,7 @@
         w_out,
         grad_partial[0],
     )
-    parts = grows // 32
+    parts = grows // 16
     mixed, grad_sum = pl.pallas_call(
         spread,
         out_shape=(

time: 128 us -> 127 us (level)
    pallas_call x1, Pallas kernels: 123 us -> 121 us  [body(): pl.pallas_call(functools.partial(kernel, n, groups), out_shape=(pltpu.VME...]
where the time goes in v2:
time: 127 us; the launch traced here: 126 us
  Pallas kernels  126 us (99%)
    pallas_call x1, Pallas kernels, body(): pl.pallas_call(functools.partial(kernel, n, groups), out_shape=(pltpu.VME...  121 us
    pallas_call x1, Pallas kernels, body(): pl.pallas_call(spread, out_shape=(jax.ShapeDtypeStruct((rows, width), bf1...  4.59 us

profile of v2, /device:TPU:0, one launch (start us, length us, event | category | flops | bytes accessed | tf_op | source)
XLA Modules:
  0.0 126.3 jit_solution(3612198828120550819)
XLA Ops:
  0.6 121.1 %shard_map.77 = (bf16[128,5120]{1,0:T(8,128)(2,1)S(1)}, bf16[512,5120]{1,0:T(8,128)(2,1)S(1)}) custom-call(bf16[128,5120]{1,0:T(8,128)(2,1)} %bitcast.8, f32[1,5120]{1,0:T(1,128)} %bitcast.10, f32[1,5120]{1,0:T(1,128)} %bitcast.11, bf16[3,5120,512]{2,1,0:T(8,128)(2,1)} %bitcast.6, bf16[512,5120]{1,0:T(8,128)(2,1)} %wo_hbm.1, bf16[512,5120]{1,0:T(8,128)(2,1)} %bitcast.7), custom_call_target="tpu_custom_call" | custom-call | flops 171798691840 | bytes 300000000 | tf_op jit(solution)/shard_map/pallas_call | solution.py:715
  121.7 4.6 %shard_map.78 = (bf16[128,5120]{1,0:T(8,128)(2,1)}, f32[512,5120]{1,0:T(8,128)}) custom-call(bf16[128,5120]{1,0:T(8,128)(2,1)S(1)} %get-tuple-element.6.mixed, bf16[512,5120]{1,0:T(8,128)(2,1)S(1)} %get-tuple-element.7.total), custom_call_target="tpu_custom_call" | custom-call | flops 2621440 | bytes 15728640 | tf_op jit(solution)/shard_map/pallas_call | solution.py:766

commit v3 on v2

--- a/solution.py
+++ b/solution.py
@@ -31,12 +31,12 @@
     wq,
     wo,
     tok,
-    tok_mate,
     blocks,
     theirs,
     stage,
     chain,
-    fin,
+    cross,
+    other,
     qkv,
     ctx,
     income,
@@ -51,8 +51,10 @@
     mx_recv,
     mp_send,
     mp_recv,
-    fin_send,
-    fin_recv,
+    ot_send,
+    ot_recv,
+    xu_recv,
+    xd_recv,
     rs_send,
     rs_recv,
     ag_send,
@@ -246,11 +248,15 @@
 
     @pl.when(up > 0)
     def _():
-        pl.semaphore_signal(barrier, inc=1, device_id={"mp": above}, device_id_type=MESH)
+        for core in range(2):
+            target = 2 * (c + 1) + core
+            pl.semaphore_signal(barrier, inc=1, device_id={"mp": target}, device_id_type=MESH)
 
     @pl.when(dn > 0)
     def _():
-        pl.semaphore_signal(barrier, inc=1, device_id={"mp": below}, device_id_type=MESH)
+        for core in range(2):
+            target = 2 * (c - 1) + core
+            pl.semaphore_signal(barrier, inc=1, device_id={"mp": target}, device_id_type=MESH)
 
     for i in range(bits):
         pl.semaphore_signal(
@@ -290,11 +296,6 @@
         at = blocks.at[slot, :, side(h)]
         return remote(at, at, own_send.at[pieces], own_recv.at[pieces], mate)
 
-    def raw(h):
-        return remote(
-            tok.at[:, side(h)], tok_mate, own_send.at[pieces + 1], own_recv.at[pieces + 1], mate
-        )
-
     def hop_up(slot, j, p):
         at = blocks.at[slot, lines(p), side(s)]
         return remote(at, at, up_send.at[j], up_recv.at[j, p], above)
@@ -321,6 +322,49 @@
             below,
         )
 
+    def add_cross_up(slot, j, p):
+        return remote(
+            theirs.at[slot, :, sub(p)],
+            cross.at[0, :, sub(p)],
+            up_send.at[j],
+            xu_recv.at[p],
+            2 * (c + 1) + 1 - s,
+        )
+
+    def add_cross_dn(slot, j, p):
+        return remote(
+            theirs.at[slot, :, sub(p)],
+            cross.at[1, :, sub(p)],
+            dn_send.at[j],
+            xd_recv.at[p],
+            2 * (c - 1) + 1 - s,
+        )
+
+    def pass_up(slot, j, p):
+        turn = jnp.where(slot == 2 * (c + 1) + 1 - s, 1, 0)
+
+        @pl.when(turn == 1)
+        def _():
+            add_cross_up(slot, j, p).start()
+
+        @pl.when(turn == 0)
+        def _():
+            add_up(slot, j, p).start()
+
+    def pass_dn(slot, j, p):
+        turn = jnp.where(slot == 2 * (c - 1) + 1 - s, 1, 0)
+
+        @pl.when(turn == 1)
+        def _():
+            add_cross_dn(slot, j, p).start()
+
+        @pl.when(turn == 0)
+        def _():
+            add_dn(slot, j, p).start()
+
+    def reveal():
+        return remote(theirs.at[mate], other, ot_send.at[0], ot_recv.at[0], mate)
+
     def to_mate(slot, p):
         at = blocks.at[slot, lines(p), side(s)]
         return remote(at, at, mx_send.at[slot], mx_recv.at[slot], mate)
@@ -342,7 +386,7 @@
             hop_dn(2 * c, 0, p).start()
 
     norm(0)
-    pl.semaphore_wait(barrier, 1 + up + dn + bits)
+    pl.semaphore_wait(barrier, 1 + 2 * up + 2 * dn + bits)
     for h in range(2):
         scatter(h, 0).start()
 
@@ -361,7 +405,6 @@
 
     lax.fori_loop(0, pieces, opening, 0)
     rest(me, s).start()
-    raw(1 - s).start()
 
     def opening_mate(p, carry):
         own(mate, s, p).wait_recv()
@@ -378,18 +421,18 @@
     def _():
         chain[chain_up(c, 2 * c), :, :] = jnp.zeros((rows, half), bf16)
         chain[chain_up(c, slots - 1), :, :] = jnp.zeros((rows, half), bf16)
+        cross[0, :, :] = jnp.zeros((rows, half), bf16)
 
     @pl.when(up == 0)
     def _():
         chain[chain_dn(c, 2 * high), :, :] = jnp.zeros((rows, half), bf16)
         chain[chain_dn(c, slots - 1), :, :] = jnp.zeros((rows, half), bf16)
+        cross[1, :, :] = jnp.zeros((rows, half), bf16)
 
     rest(mate, 1 - s).wait_recv()
-    raw(s).wait_recv()
     for p in range(pieces):
         own(me, 1 - s, p).wait_send()
     rest(me, s).wait_send()
-    raw(1 - s).wait_send()
     load_q.wait()
     load_o.wait()
 
@@ -438,23 +481,17 @@
     def mine(slot, p):
         return blocks[slot, :, cols(1 - s, p)].astype(f32) + theirs[slot, :, sub(p)].astype(f32)
 
-    def finish(slot, p, foreign):
+    def finish(p):
+        from_dn = chain[chain_up(c, jnp.where(s == 0, 2 * c, slots - 1)), :, sub(p)]
+        from_up = chain[chain_dn(c, jnp.where(s == 0, 2 * high, slots - 1)), :, sub(p)]
+        value = mine(me, p) + from_dn.astype(f32) + from_up.astype(f32)
+        out[:, cols(s, p)] = (tok[:, cols(s, p)].astype(f32) + value).astype(bf16)
         value = (
-            mine(slot, p)
-            + chain[chain_up(c, jnp.where(slot % 2 == 0, 2 * c, slots - 1)), :, sub(p)].astype(f32)
-            + chain[chain_dn(c, jnp.where(slot % 2 == 0, 2 * high, slots - 1)), :, sub(p)].astype(f32)
-        )
-        if foreign:
-            fin[:, sub(p)] = (tok_mate[:, sub(p)].astype(f32) + value).astype(bf16)
-            give(p).start()
-        else:
-            out[:, cols(s, p)] = (tok[:, cols(s, p)].astype(f32) + value).astype(bf16)
-
-    def give(p):
-        return remote(fin.at[:, sub(p)], out.at[:, cols(s, p)], fin_send.at[p], fin_recv.at[p], mate)
-
-    def take(p):
-        return remote(fin.at[:, sub(p)], out.at[:, cols(1 - s, p)], fin_send.at[p], fin_recv.at[p], mate)
+            other[:, sub(p)].astype(f32)
+            + cross[0, :, sub(p)].astype(f32)
+            + cross[1, :, sub(p)].astype(f32)
+        )
+        out[:, cols(1 - s, p)] = (tok[:, cols(1 - s, p)].astype(f32) + value).astype(bf16)
 
     top = 1 - up
 
@@ -489,18 +526,29 @@
 
         last = jnp.where(j == slots - 1, 1, 0)
 
+        @pl.when(jnp.where(j == 1, 1, 0) * jnp.where(p == 0, 1, 0) > 0)
+        def _():
+            share(0, mate).wait_recv()
+
+            def one(q, carry):
+                theirs[mate, :, sub(q)] = mine(mate, q).astype(bf16)
+                return carry
+
+            lax.fori_loop(0, pieces, one, 0)
+            reveal().start()
+
         @pl.when(last * jnp.where(p == 0, 1, 0) > 0)
         def _():
-            share(0, 2 * c).wait_recv()
-            share(0, 2 * c + 1).wait_recv()
-            for ab in range(2):
-                @pl.when(s == ab)
-                def _():
-                    def one(q, carry):
-                        finish(2 * c, q, ab == 1)
-                        return carry
-
-                    lax.fori_loop(0, pieces, one, 0)
+            share(0, me).wait_recv()
+            reveal().wait_recv()
+
+            @pl.when(s == 0)
+            def _():
+                def one(q, carry):
+                    finish(q)
+                    return carry
+
+                lax.fori_loop(0, pieces, one, 0)
 
         @pl.when(dn > 0)
         def _():
@@ -519,13 +567,20 @@
             def _():
                 image = sum_into_up(c, j)
                 at = chain_up(c, j)
-                remote(
-                    theirs.at[image, :, sub(p)],
-                    chain.at[at, :, sub(p)],
-                    up_send.at[j],
-                    up_recv.at[j, p],
-                    above,
-                ).wait_recv()
+
+                @pl.when(image != mate)
+                def _():
+                    remote(
+                        theirs.at[image, :, sub(p)],
+                        chain.at[at, :, sub(p)],
+                        up_send.at[j],
+                        up_recv.at[j, p],
+                        above,
+                    ).wait_recv()
+
+                @pl.when(image == me)
+                def _():
+                    add_cross_up(image, j, p).wait_recv()
 
                 @pl.when(image >= 2 * c + 2)
                 def _():
@@ -536,7 +591,7 @@
                     theirs[image, :, sub(p)] = (
                         mine(image, p) + chain[at, :, sub(p)].astype(f32)
                     ).astype(bf16)
-                    add_up(image, j + 1, p).start()
+                    pass_up(image, j + 1, p)
 
         @pl.when(up > 0)
         def _():
@@ -555,13 +610,20 @@
             def _():
                 image = sum_into_dn(c, j)
                 at = chain_dn(c, j)
-                remote(
-                    theirs.at[image, :, sub(p)],
-                    chain.at[at, :, sub(p)],
-                    dn_send.at[j],
-                    dn_recv.at[j, p],
-                    below,
-                ).wait_recv()
+
+                @pl.when(image != mate)
+                def _():
+                    remote(
+                        theirs.at[image, :, sub(p)],
+                        chain.at[at, :, sub(p)],
+                        dn_send.at[j],
+                        dn_recv.at[j, p],
+                        below,
+                    ).wait_recv()
+
+                @pl.when(image == me)
+                def _():
+                    add_cross_dn(image, j, p).wait_recv()
 
                 @pl.when(image < 2 * c)
                 def _():
@@ -572,7 +634,7 @@
                     theirs[image, :, sub(p)] = (
                         mine(image, p) + chain[at, :, sub(p)].astype(f32)
                     ).astype(bf16)
-                    add_dn(image, j + 1, p).start()
+                    pass_dn(image, j + 1, p)
 
         @pl.when(up * jnp.where(p == 0, 1, 0) * jnp.where(j == 2 * c, 1, 0) > 0)
         def _():
@@ -593,7 +655,7 @@
 
             def one(q, carry):
                 theirs[image, :, sub(q)] = mine(image, q).astype(bf16)
-                add_up(image, j + 1, q).start()
+                pass_up(image, j + 1, q)
                 return carry
 
             lax.fori_loop(0, pieces, one, 0)
@@ -605,15 +667,14 @@
 
             def one(q, carry):
                 theirs[image, :, sub(q)] = mine(image, q).astype(bf16)
-                add_dn(image, j + 1, q).start()
+                pass_dn(image, j + 1, q)
                 return carry
 
             lax.fori_loop(0, pieces, one, 0)
 
-        for ab in range(2):
-            @pl.when(last * jnp.where(s == ab, 1, 0) > 0)
-            def _():
-                finish(2 * c + 1, p, ab == 0)
+        @pl.when(last * s > 0)
+        def _():
+            finish(p)
 
         for e, when in enumerate(times):
             @pl.when(j * pieces + p == when)
@@ -638,9 +699,6 @@
 
     lax.fori_loop(0, slots, slot_loop, 0)
 
-    for p in range(pieces):
-        take(p).wait_recv()
-
     def drain(j, carry):
         @pl.when(up > 0)
         def _():
@@ -661,8 +719,7 @@
         return carry
 
     lax.fori_loop(0, slots, drain, 0)
-    for p in range(pieces):
-        give(p).wait_send()
+    reveal().wait_send()
     for h in range(2):
         for i in range(bits):
             scatter(h, i).wait_send()
@@ -721,18 +778,18 @@
             pltpu.VMEM((3, width, inner), bf16),
             pltpu.VMEM((inner, width), bf16),
             pltpu.VMEM((rows, width), bf16),
-            pltpu.VMEM((rows, half), bf16),
             pltpu.VMEM((n, rows, width), bf16),
             pltpu.VMEM((n, rows, half), bf16),
             pltpu.VMEM((2, rows, half), bf16),
             pltpu.VMEM((slots + 2, rows, half), bf16),
+            pltpu.VMEM((2, rows, half), bf16),
             pltpu.VMEM((rows, half), bf16),
             pltpu.VMEM((3, rows, inner), bf16),
             pltpu.VMEM((rows, inner), bf16),
             pltpu.VMEM((2, income, width), bf16),
             dma((5,)),
-            dma((pieces + 2,)),
-            dma((pieces + 2,)),
+            dma((pieces + 1,)),
+            dma((pieces + 1,)),
             dma((slots,)),
             dma((slots, pieces)),
             dma((slots,)),
@@ -741,6 +798,8 @@
             dma((n,)),
             dma((2,)),
             dma((n,)),
+            dma((1,)),
+            dma((1,)),
             dma((pieces,)),
             dma((pieces,)),
             dma((2, bits)),

time: 127 us -> 127 us (level)
  no operation moved by 1% of the time
where the time goes in v3:
time: 127 us; the launch traced here: 126 us
  Pallas kernels  126 us (99%)
    pallas_call x1, Pallas kernels, body(): pl.pallas_call(functools.partial(kernel, n, groups), out_shape=(pltpu.VME...  121 us
    pallas_call x1, Pallas kernels, body(): pl.pallas_call(spread, out_shape=(jax.ShapeDtypeStruct((rows, width), bf1...  4.59 us

profile of v3, /device:TPU:0, one launch (start us, length us, event | category | flops | bytes accessed | tf_op | source)
XLA Modules:
  0.0 126.3 jit_solution(18334790366643472966)
XLA Ops:
  0.6 121.1 %shard_map.77 = (bf16[128,5120]{1,0:T(8,128)(2,1)S(1)}, bf16[512,5120]{1,0:T(8,128)(2,1)S(1)}) custom-call(bf16[128,5120]{1,0:T(8,128)(2,1)} %bitcast.8, f32[1,5120]{1,0:T(1,128)} %bitcast.10, f32[1,5120]{1,0:T(1,128)} %bitcast.11, bf16[3,5120,512]{2,1,0:T(8,128)(2,1)} %bitcast.6, bf16[512,5120]{1,0:T(8,128)(2,1)} %wo_hbm.1, bf16[512,5120]{1,0:T(8,128)(2,1)} %bitcast.7), custom_call_target="tpu_custom_call" | custom-call | flops 171798691840 | bytes 300000000 | tf_op jit(solution)/shard_map/pallas_call | solution.py:772
  121.7 4.6 %shard_map.78 = (bf16[128,5120]{1,0:T(8,128)(2,1)}, f32[512,5120]{1,0:T(8,128)}) custom-call(bf16[128,5120]{1,0:T(8,128)(2,1)S(1)} %get-tuple-element.6.mixed, bf16[512,5120]{1,0:T(8,128)(2,1)S(1)} %get-tuple-element.7.total), custom_call_target="tpu_custom_call" | custom-call | flops 2621440 | bytes 15728640 | tf_op jit(solution)/shard_map/pallas_call | solution.py:825

commit v4 on v3

--- a/solution.py
+++ b/solution.py
@@ -82,6 +82,26 @@
     f32 = jnp.float32
     bf16 = jnp.bfloat16
 
+    barrier = pltpu.get_barrier_semaphore()
+    pl.semaphore_signal(barrier, inc=1, device_id={"mp": mate}, device_id_type=MESH)
+
+    @pl.when(up > 0)
+    def _():
+        for core in range(2):
+            target = 2 * (c + 1) + core
+            pl.semaphore_signal(barrier, inc=1, device_id={"mp": target}, device_id_type=MESH)
+
+    @pl.when(dn > 0)
+    def _():
+        for core in range(2):
+            target = 2 * (c - 1) + core
+            pl.semaphore_signal(barrier, inc=1, device_id={"mp": target}, device_id_type=MESH)
+
+    for i in range(bits):
+        pl.semaphore_signal(
+            barrier, inc=1, device_id={"dp": group + (1 << i) * (1 - 2 * ((group // (1 << i)) % 2))}, device_id_type=MESH
+        )
+
     def remote(src, dst, send, recv, target):
         return pltpu.make_async_remote_copy(
             src_ref=src,
@@ -243,26 +263,6 @@
         at_tick += -(-lines // (rows * wide)) + 1
         times.append(min(at_tick, slots * pieces - 2 * bits + e))
 
-    barrier = pltpu.get_barrier_semaphore()
-    pl.semaphore_signal(barrier, inc=1, device_id={"mp": mate}, device_id_type=MESH)
-
-    @pl.when(up > 0)
-    def _():
-        for core in range(2):
-            target = 2 * (c + 1) + core
-            pl.semaphore_signal(barrier, inc=1, device_id={"mp": target}, device_id_type=MESH)
-
-    @pl.when(dn > 0)
-    def _():
-        for core in range(2):
-            target = 2 * (c - 1) + core
-            pl.semaphore_signal(barrier, inc=1, device_id={"mp": target}, device_id_type=MESH)
-
-    for i in range(bits):
-        pl.semaphore_signal(
-            barrier, inc=1, device_id={"dp": partner(0, i)[0]}, device_id_type=MESH
-        )
-
     load_t.wait()
     load_q.start()
     load_o.start()
@@ -400,6 +400,14 @@
         @pl.when(s == 0)
         def _():
             first_hops(p)
+
+        @pl.when(s * up * jnp.where(p == 0, 1, 0) > 0)
+        def _():
+            hop_up(2 * c + 1, 2 * c + 1, 0).start()
+
+        @pl.when(s * dn * jnp.where(p == 0, 1, 0) > 0)
+        def _():
+            hop_dn(2 * c + 1, 2 * high + 1, 0).start()
 
         return carry
 
@@ -550,6 +558,32 @@
 
                 lax.fori_loop(0, pieces, one, 0)
 
+        begin = jnp.where(p == 2, 1, 0) * jnp.minimum(j, 1) * (1 - last)
+
+        @pl.when(begin * (1 - dn) * up > 0)
+        def _():
+            image = sum_into_up(c + 1, j + 1)
+            share(0, image).wait_recv()
+
+            def one(q, carry):
+                theirs[image, :, sub(q)] = mine(image, q).astype(bf16)
+                pass_up(image, j + 1, q)
+                return carry
+
+            lax.fori_loop(0, pieces, one, 0)
+
+        @pl.when(begin * (1 - up) * dn > 0)
+        def _():
+            image = sum_into_dn(c - 1, j + 1)
+            share(0, image).wait_recv()
+
+            def one(q, carry):
+                theirs[image, :, sub(q)] = mine(image, q).astype(bf16)
+                pass_dn(image, j + 1, q)
+                return carry
+
+            lax.fori_loop(0, pieces, one, 0)
+
         @pl.when(dn > 0)
         def _():
             @pl.when(j < 2 * c)
@@ -638,39 +672,21 @@
 
         @pl.when(up * jnp.where(p == 0, 1, 0) * jnp.where(j == 2 * c, 1, 0) > 0)
         def _():
-            for q in range(pieces):
+            @pl.when(s == 0)
+            def _():
+                hop_up(2 * c + 1, 2 * c + 1, 0).start()
+
+            for q in range(1, pieces):
                 hop_up(2 * c + 1, 2 * c + 1, q).start()
 
         @pl.when(dn * jnp.where(p == 0, 1, 0) * jnp.where(j == 2 * high, 1, 0) > 0)
         def _():
-            for q in range(pieces):
+            @pl.when(s == 0)
+            def _():
+                hop_dn(2 * c + 1, 2 * high + 1, 0).start()
+
+            for q in range(1, pieces):
                 hop_dn(2 * c + 1, 2 * high + 1, q).start()
-
-        begin = jnp.where(p == 3, 1, 0) * jnp.minimum(j, 1) * (1 - last)
-
-        @pl.when(begin * (1 - dn) * up > 0)
-        def _():
-            image = sum_into_up(c + 1, j + 1)
-            share(0, image).wait_recv()
-
-            def one(q, carry):
-                theirs[image, :, sub(q)] = mine(image, q).astype(bf16)
-                pass_up(image, j + 1, q)
-                return carry
-
-            lax.fori_loop(0, pieces, one, 0)
-
-        @pl.when(begin * (1 - up) * dn > 0)
-        def _():
-            image = sum_into_dn(c - 1, j + 1)
-            share(0, image).wait_recv()
-
-            def one(q, carry):
-                theirs[image, :, sub(q)] = mine(image, q).astype(bf16)
-                pass_dn(image, j + 1, q)
-                return carry
-
-            lax.fori_loop(0, pieces, one, 0)
 
         @pl.when(last * s > 0)
         def _():

time: 127 us -> 125 us (0.984)
  Pallas kernels: 126 us -> 123 us
    pallas_call x1, Pallas kernels: 121 us -> 118 us  [body(): pl.pallas_call(functools.partial(kernel, n, groups), out_shape=(pltpu.VME...]
where the time goes in v4:
time: 125 us; the launch traced here: 123 us
  Pallas kernels  123 us (98%)
    pallas_call x1, Pallas kernels, body(): pl.pallas_call(functools.partial(kernel, n, groups), out_shape=(pltpu.VME...  118 us
    pallas_call x1, Pallas kernels, body(): pl.pallas_call(spread, out_shape=(jax.ShapeDtypeStruct((rows, width), bf1...  4.59 us

profile of v4, /device:TPU:0, one launch (start us, length us, event | category | flops | bytes accessed | tf_op | source)
XLA Modules:
  0.0 123.2 jit_solution(12528131159264198373)
XLA Ops:
  0.6 118.0 %shard_map.77 = (bf16[128,5120]{1,0:T(8,128)(2,1)S(1)}, bf16[512,5120]{1,0:T(8,128)(2,1)S(1)}) custom-call(bf16[128,5120]{1,0:T(8,128)(2,1)} %bitcast.8, f32[1,5120]{1,0:T(1,128)} %bitcast.10, f32[1,5120]{1,0:T(1,128)} %bitcast.11, bf16[3,5120,512]{2,1,0:T(8,128)(2,1)} %bitcast.6, bf16[512,5120]{1,0:T(8,128)(2,1)} %wo_hbm.1, bf16[512,5120]{1,0:T(8,128)(2,1)} %bitcast.7), custom_call_target="tpu_custom_call" | custom-call | flops 171798691840 | bytes 300000000 | tf_op jit(solution)/shard_map/pallas_call | solution.py:788
  118.7 4.6 %shard_map.78 = (bf16[128,5120]{1,0:T(8,128)(2,1)}, f32[512,5120]{1,0:T(8,128)}) custom-call(bf16[128,5120]{1,0:T(8,128)(2,1)S(1)} %get-tuple-element.6.mixed, bf16[512,5120]{1,0:T(8,128)(2,1)S(1)} %get-tuple-element.7.total), custom_call_target="tpu_custom_call" | custom-call | flops 2621440 | bytes 15728640 | tf_op jit(solution)/shard_map/pallas_call | solution.py:841

commit v5 on v4

--- a/solution.py
+++ b/solution.py
@@ -514,6 +514,28 @@
         slot = jnp.where(from_above == 1, gather_above(a), gather_below(a))
         return exists, jnp.where(j == 0, 2 * c + k, slot)
 
+    def drain(j, carry):
+        @pl.when(up > 0)
+        def _():
+            remote(
+                blocks.at[0, :, side(s)], blocks.at[0, :, side(s)], up_send.at[j], up_recv.at[0, 0], above
+            ).wait_send()
+
+        @pl.when(dn > 0)
+        def _():
+            remote(
+                blocks.at[0, :, side(s)], blocks.at[0, :, side(s)], dn_send.at[j], dn_recv.at[0, 0], below
+            ).wait_send()
+
+        return carry
+
+    def drain_mate(image, carry):
+        @pl.when(image // 2 != c)
+        def _():
+            from_mate(image).wait_send()
+
+        return carry
+
     def tick(j, p):
         k = p // 2
         exists, slot = candidate(j, k)
@@ -688,6 +710,12 @@
             for q in range(1, pieces):
                 hop_dn(2 * c + 1, 2 * high + 1, q).start()
 
+        @pl.when(last * jnp.where(p == 1, 1, 0) > 0)
+        def _():
+            lax.fori_loop(0, slots - 1, drain, 0)
+            lax.fori_loop(0, n, drain_mate, 0)
+            reveal().wait_send()
+
         @pl.when(last * s > 0)
         def _():
             finish(p)
@@ -715,27 +743,7 @@
 
     lax.fori_loop(0, slots, slot_loop, 0)
 
-    def drain(j, carry):
-        @pl.when(up > 0)
-        def _():
-            remote(
-                blocks.at[0, :, side(s)], blocks.at[0, :, side(s)], up_send.at[j], up_recv.at[0, 0], above
-            ).wait_send()
-
-        @pl.when(dn > 0)
-        def _():
-            remote(
-                blocks.at[0, :, side(s)], blocks.at[0, :, side(s)], dn_send.at[j], dn_recv.at[0, 0], below
-            ).wait_send()
-
-        @pl.when(j // 2 != c)
-        def _():
-            from_mate(j).wait_send()
-
-        return carry
-
-    lax.fori_loop(0, slots, drain, 0)
-    reveal().wait_send()
+    drain(slots - 1, 0)
     for h in range(2):
         for i in range(bits):
             scatter(h, i).wait_send()
@@ -837,7 +845,7 @@
         w_out,
         grad_partial[0],
     )
-    parts = grows // 16
+    parts = grows // 64
     mixed, grad_sum = pl.pallas_call(
         spread,
         out_shape=(

time: 125 us -> 125 us (level)
  no operation moved by 1% of the time
where the time goes in v5:
time: 125 us; the launch traced here: 123 us
  Pallas kernels  122 us (98%)
    pallas_call x1, Pallas kernels, body(): pl.pallas_call(functools.partial(kernel, n, groups), out_shape=(pltpu.VME...  118 us
    pallas_call x1, Pallas kernels, body(): pl.pallas_call(spread, out_shape=(jax.ShapeDtypeStruct((rows, width), bf1...  4.44 us

profile of v5, /device:TPU:0, one launch (start us, length us, event | category | flops | bytes accessed | tf_op | source)
XLA Modules:
  0.0 123.1 jit_solution(13054754044814925412)
XLA Ops:
  0.6 118.0 %shard_map.77 = (bf16[128,5120]{1,0:T(8,128)(2,1)S(1)}, bf16[512,5120]{1,0:T(8,128)(2,1)S(1)}) custom-call(bf16[128,5120]{1,0:T(8,128)(2,1)} %bitcast.8, f32[1,5120]{1,0:T(1,128)} %bitcast.10, f32[1,5120]{1,0:T(1,128)} %bitcast.11, bf16[3,5120,512]{2,1,0:T(8,128)(2,1)} %bitcast.6, bf16[512,5120]{1,0:T(8,128)(2,1)} %wo_hbm.1, bf16[512,5120]{1,0:T(8,128)(2,1)} %bitcast.7), custom_call_target="tpu_custom_call" | custom-call | flops 171798691840 | bytes 300000000 | tf_op jit(solution)/shard_map/pallas_call | solution.py:796
  118.6 4.4 %shard_map.78 = (bf16[128,5120]{1,0:T(8,128)(2,1)}, f32[512,5120]{1,0:T(8,128)}) custom-call(bf16[128,5120]{1,0:T(8,128)(2,1)S(1)} %get-tuple-element.6.mixed, bf16[512,5120]{1,0:T(8,128)(2,1)S(1)} %get-tuple-element.7.total), custom_call_target="tpu_custom_call" | custom-call | flops 2621440 | bytes 15728640 | tf_op jit(solution)/shard_map/pallas_call | solution.py:849
